TPU v7x, 256 devices: a whole 4x4x8 slice. The times are simulated.
256 devices in a mesh: gx: 16 (over z, x_lo), gy: 16 (over y, x_hi, core).
Axes of the slice: x: 4 (x_hi: 2, x_lo: 2; x = x_hi * 2 + x_lo), y: 4, z: 8, core: 2. Of those that a mesh axis runs over, the one named last changes fastest.
Arguments:
- gradient: float32 [2048, 512], P('gx', 'gy'), may hold values from -6 to 6
- stat_old: float32 [2048, 2048], P('gx', 'gy'), may hold values from -1.001 to 1.001, as said below
Outputs:
- statistic: float32 [2048, 2048], P('gx', 'gy')
- inverse_root: float32 [2048, 2048], P('gx', 'gy')
Inputs may be any that keep to these rules, and one draw needn't show every extreme that they name: stat_old is symmetric positive semidefinite with unit diagonal, the Gram matrix of 2048 unit-length rows of 512 entries.
All inputs are finite; a program needn't handle non-finite values.
Results may differ from a plain program's by a relative error of at most 0.0003.
Values sent between devices are 32-bit elements.
A program may use at most 64 MiB of HBM per device.

v0:
```python
import jax
import jax.numpy as jnp
from jax import lax
from jax.sharding import Mesh
from jax.sharding import PartitionSpec as P

GY = ("gy_0", "gy_1", "gy_2")
GX = ("gx_0", "gx_1")
GX_GY = ("gx_0", "gx_1", "gy_0", "gy_1", "gy_2")


def gather_axes(array, axes, dim):
    filled = array
    for number in range(len(axes) - 1, -1, -1):
        filled = lax.all_gather(filled, axes[number], axis=dim, tiled=True)
    return filled


def folded(array, axes, dim, take_in, carry):
    everything = jax.tree.map(lambda part: gather_axes(part, axes, dim), array)
    return take_in(carry, everything, jnp.int32(0))


def spread(array, axes, root):
    array = jnp.where(lax.axis_index(axes) == root, array, jnp.zeros_like(array))
    for axis in axes:
        array = lax.psum(array, axis)
    return array


def over_axes(array, axes):
    for axis in axes:
        array = lax.psum(array, axis)
    return array


def matmul(leading, trailing):
    return jnp.dot(
        leading, trailing, preferred_element_type=jnp.float32, precision=lax.Precision.HIGHEST
    )


def panels(factor_one, factor_two):
    whole_row = lax.all_gather(factor_one, GY, axis=1, tiled=True)

    def accumulate(running, shard_rows, first_row):
        matching = lax.dynamic_slice_in_dim(whole_row, first_row, shard_rows.shape[0], 1)
        return running + matmul(matching, shard_rows)

    empty = jnp.zeros((factor_one.shape[0], factor_two.shape[1]), jnp.float32)
    return folded(factor_two, GX, 0, accumulate, empty)


def product(factor_one, factor_two):
    return panels(factor_one, factor_two)


def local(gradient, stat_old):
    count_rows = lax.axis_size(GX)
    count_cols = lax.axis_size(GY)
    factor = count_rows // count_cols
    piece_width = stat_old.shape[0]
    row_index = lax.axis_index(GX)
    col_index = lax.axis_index(GY)
    panel_rows = lax.all_gather(gradient, GY, axis=1, tiled=True)
    outer_parts = []
    for member in range(factor):
        column_rows = spread(panel_rows, GX, col_index * factor + member)
        outer_parts.append(matmul(panel_rows, column_rows.T))
    outer = jnp.concatenate(outer_parts, axis=1) / panel_rows.shape[1]
    statistic = 0.9 * stat_old + outer
    squares = over_axes(jnp.sum(statistic * statistic), GX_GY)
    divisor = 2.0 * jnp.sqrt(squares / (piece_width * count_rows))
    global_rows = row_index * piece_width + lax.broadcasted_iota(jnp.int32, stat_old.shape, 0)
    global_cols = col_index * (factor * piece_width) + lax.broadcasted_iota(
        jnp.int32, stat_old.shape, 1
    )
    identity = (global_rows == global_cols).astype(jnp.float32)
    normed = statistic / divisor
    first_step = 1.5 * identity - 0.5 * normed
    root_half = product(normed, first_step)
    product_mid = product(first_step, root_half)
    second_step = 1.5 * identity - 0.5 * product_mid
    inverse_root = product(second_step, first_step)
    return (statistic, inverse_root)


def solution(mesh):
    torus = Mesh(mesh.devices.reshape(8, 2, 4, 2, 2), ("gx_0", "gx_1", "gy_0", "gy_1", "gy_2"))
    placed = (P(GX, GY), P(GX, GY))
    return jax.shard_map(
        local, mesh=torus, in_specs=placed, out_specs=(P(GX, GY), P(GX, GY)), check_vma=False
    )
```

profile of v0, /device:TPU:1, one launch (start us, length us, event | category | flops | bytes accessed | tf_op | source)
XLA Modules:
  0.0 435.5 jit_solution(8363940582427046131)
XLA Ops:
  7.2 0.0 copy-start.3
  7.2 0.0 all-reduce.3.cloned.1.call-start
  7.2 0.7 copy-done.3
  7.9 26.8 %all_gather.26 = f32[128,512]{0,1:T(8,128)S(1)} all-gather(f32[128,32]{0,1:T(8,128)S(1)} %copy-done.3), channel_id=1, replica_groups=mesh['gx_0'=8,'gx_1'=2,'gy_0'=4,'gy_1'=2,'gy_2'=2] {'gy_0','gy_1','gy_2'}, dimensions={1}, use_global_device_ids=true | all-gather | bytes 278528 | tf_op jit(solution)/shard_map/all_gather | solution.py:65
  34.6 0.7 broadcast_select_fusion
  35.4 0.0 all-reduce.3.cloned.1.call-update
  35.4 0.0 all-reduce.5.cloned.1.call-start
  35.4 65.4 %all-reduce.3.cloned.1.call-done = f32[128,512]{0,1:T(8,128)} async-done(((f32[128,512]{0,1:T(8,128)}), f32[128,512]{0,1:T(8,128)}) %all-reduce.3.cloned.1.call-update) | async-done | bytes 262160 | tf_op jit(solution)/shard_map/psum | solution.py:27
  100.8 0.0 copy-start.2
  100.8 0.0 all-reduce.5.cloned.1.call-update
  100.8 0.0 all-gather.10.cloned.1.call-start
  100.9 0.8 copy-done.2
  101.6 0.1 copy.4
  101.7 39.7 %all-reduce.5.cloned.1.call-done = f32[128,512]{0,1:T(8,128)} async-done(((f32[128,512]{0,1:T(8,128)}), f32[128,512]{0,1:T(8,128)}) %all-reduce.5.cloned.1.call-update) | async-done | bytes 262160 | tf_op jit(solution)/shard_map/psum | solution.py:27
  141.4 2.1 multiply_reduce_fusion
  143.6 14.6 %psum.51 = f32[]{:T(128)} all-reduce(f32[]{:T(128)} %get-tuple-element.6), channel_id=1, replica_groups=mesh['gx_0'=8,'gx_1'=2,'gy_0'=4,'gy_1'=2,'gy_2'=2] {'gx_0'}, use_global_device_ids=true, to_apply=%region_3.4 | all-reduce | flops 1 | bytes 8 | tf_op jit(solution)/shard_map/psum | solution.py:33
  158.1 4.4 %psum.52 = f32[]{:T(128)} all-reduce(f32[]{:T(128)} %psum.51), channel_id=1, replica_groups=mesh['gx_0'=8,'gx_1'=2,'gy_0'=4,'gy_1'=2,'gy_2'=2] {'gx_1'}, use_global_device_ids=true, to_apply=%region_4.5 | all-reduce | flops 1 | bytes 8 | tf_op jit(solution)/shard_map/psum | solution.py:33
  162.5 9.1 %psum.53 = f32[]{:T(128)} all-reduce(f32[]{:T(128)} %psum.52), channel_id=1, replica_groups=mesh['gx_0'=8,'gx_1'=2,'gy_0'=4,'gy_1'=2,'gy_2'=2] {'gy_0'}, use_global_device_ids=true, to_apply=%region_5.6 | all-reduce | flops 1 | bytes 8 | tf_op jit(solution)/shard_map/psum | solution.py:33
  171.6 5.9 %psum.54 = f32[]{:T(128)} all-reduce(f32[]{:T(128)} %psum.53), channel_id=1, replica_groups=mesh['gx_0'=8,'gx_1'=2,'gy_0'=4,'gy_1'=2,'gy_2'=2] {'gy_1'}, use_global_device_ids=true, to_apply=%region_6.7 | all-reduce | flops 1 | bytes 8 | tf_op jit(solution)/shard_map/psum | solution.py:33
  177.5 11.8 %psum.55 = f32[]{:T(128)} all-reduce(f32[]{:T(128)} %psum.54), channel_id=1, replica_groups=mesh['gx_0'=8,'gx_1'=2,'gy_0'=4,'gy_1'=2,'gy_2'=2] {'gy_2'}, use_global_device_ids=true, to_apply=%region_7.8 | all-reduce | flops 1 | bytes 8 | tf_op jit(solution)/shard_map/psum | solution.py:33
  190.0 0.6 select_subtract_fusion
  190.6 0.0 copy-start.1
  190.6 3.9 all_gather.29
  194.5 0.0 copy-done.1
  194.5 0.0 all-gather.10.cloned.1.call-update
  194.5 0.0 all-gather.8.cloned.1.call-start
  194.6 0.5 all-gather.8.cloned.1.call-update
  195.1 0.0 all-gather.6.cloned.1.call-start
  195.1 0.5 all-gather.6.cloned.1.call-update
  195.7 0.0 all-gather.12.cloned.1.call-start
  195.7 29.4 %all-gather.10.cloned.1.call-done = f32[2048,128]{0,1:T(8,128)} async-done(((f32[256,128]{0,1:T(8,128)}), f32[2048,128]{0,1:T(8,128)}) %all-gather.10.cloned.1.call-update) | async-done | bytes 1048592 | tf_op jit(solution)/shard_map/all_gather | solution.py:15
  225.1 56.8 %all-gather.8.cloned.1.call-done = f32[128,2048]{0,1:T(8,128)} async-done(((f32[128,128]{0,1:T(8,128)}), f32[128,2048]{0,1:T(8,128)}) %all-gather.8.cloned.1.call-update) | async-done | bytes 1048592 | tf_op jit(solution)/shard_map/all_gather | solution.py:44
  281.9 3.4 fusion.3
  285.2 3.9 all_gather.31
  289.1 0.0 all-gather.12.cloned.1.call-update
  289.1 0.0 copy-start
  289.1 0.0 all-gather.14.cloned.1.call-start
  289.2 44.5 %all-gather.6.cloned.1.call-done = f32[128,2048]{0,1:T(8,128)} async-done(((f32[128,128]{0,1:T(8,128)}), f32[128,2048]{0,1:T(8,128)}) %all-gather.6.cloned.1.call-update) | async-done | bytes 1048592 | tf_op jit(solution)/shard_map/all_gather | solution.py:44
  333.7 33.6 %all-gather.12.cloned.1.call-done = f32[2048,128]{1,0:T(8,128)} async-done(((f32[256,128]{1,0:T(8,128)}), f32[2048,128]{1,0:T(8,128)}) %all-gather.12.cloned.1.call-update) | async-done | bytes 1048592 | tf_op jit(solution)/shard_map/all_gather | solution.py:15
  367.3 4.0 fusion
  371.3 0.0 all-gather.14.cloned.1.call-update
  371.3 0.7 copy.5
  372.0 53.0 %all-gather.14.cloned.1.call-done = f32[128,2048]{0,1:T(8,128)} async-done(((f32[128,128]{0,1:T(8,128)}), f32[128,2048]{0,1:T(8,128)}) %all-gather.14.cloned.1.call-update) | async-done | bytes 1048592 | tf_op jit(solution)/shard_map/all_gather | solution.py:44
  425.0 0.0 copy-done
  425.0 3.7 fusion.4
  (1 shorter events, 0.0 us)
Async XLA Ops:
  7.2 0.7 copy-start.3
  7.2 93.6 %all-reduce.3.cloned.1.call-start = ((), (), s32[]{:S(2)}) async-start(), calls=%async_computation | async-start | bytes 524288 | tf_op jit(solution)/shard_map/psum | solution.py:27
  35.4 106.1 %all-reduce.5.cloned.1.call-start = ((), (), s32[]{:S(2)}) async-start(), calls=%async_computation.1 | async-start | bytes 524288 | tf_op jit(solution)/shard_map/psum | solution.py:27
  100.8 0.8 copy-start.2
  100.8 124.2 %all-gather.10.cloned.1.call-start = ((), (), s32[]{:S(2)}) async-start(), calls=%async_computation.4 | async-start | bytes 1179648 | tf_op jit(solution)/shard_map/all_gather | solution.py:15
  190.6 3.9 copy-start.1
  194.5 87.3 %all-gather.8.cloned.1.call-start = ((), (), s32[]{:S(2)}) async-start(), calls=%async_computation.3 | async-start | bytes 1114112 | tf_op jit(solution)/shard_map/all_gather | solution.py:44
  195.1 138.6 %all-gather.6.cloned.1.call-start = ((), (), s32[]{:S(2)}) async-start(), calls=%async_computation.2 | async-start | bytes 1114112 | tf_op jit(solution)/shard_map/all_gather | solution.py:44
  195.7 171.6 %all-gather.12.cloned.1.call-start = ((), (), s32[]{:S(2)}) async-start(), calls=%async_computation.5 | async-start | bytes 1179648 | tf_op jit(solution)/shard_map/all_gather | solution.py:15
  289.1 135.9 %copy-start = (f32[2048,128]{0,1:T(8,128)S(1)}, f32[2048,128]{0,1:T(8,128)}, u32[]{:S(2)}) copy-start(f32[2048,128]{0,1:T(8,128)} %all-gather.10.cloned.1.call-done) | copy-start | bytes 3145732
  289.1 135.9 %all-gather.14.cloned.1.call-start = ((), (), s32[]{:S(2)}) async-start(), calls=%async_computation.6 | async-start | bytes 1114112 | tf_op jit(solution)/shard_map/all_gather | solution.py:44
Sparse Core Ops, SparseCore 0:
  35.5 65.2 all-reduce.2
  103.4 38.0 all-reduce.4
  194.6 30.4 all-gather.9
  228.3 53.5 all-gather.7
  285.0 48.6 all-gather.5
  335.4 31.8 all-gather.11
  371.4 53.5 all-gather.13
where the time goes:
time: 436 us
  waiting for transfers between devices  323 us (74%)
  blocking collectives  80.2 us (18%)
  between operations  14.9 us (3%)
  matrix products  13.2 us (3%)
    all_gather x3, waiting for transfers between devices, panels(): whole_row = lax.all_gather(factor_one, GY, axis=1, tiled=True)  154 us
    psum x2, waiting for transfers between devices, spread(): array = lax.psum(array, axis)  105 us
    all_gather x2, waiting for transfers between devices, gather_axes(): filled = lax.all_gather(filled, axes[number], axis=dim, tiled=True)  62.9 us
    psum x5, blocking collectives, over_axes(): array = lax.psum(array, axis)  45.7 us
    all_gather x1, blocking collectives, local(): panel_rows = lax.all_gather(gradient, GY, axis=1, tiled=True)  26.8 us
    dot_general x4, matrix products, matmul(): jnp.dot(leading, trailing, preferred_element_type=jnp.float32, precision=...  13.2 us
  transfers between devices with their start and end apart: 7, of which 7 were waited for; matrix products, arithmetic and copies ran while one was open for 1% of the time, Pallas kernels for 0%

commit v1 on v0

--- a/solution.py
+++ b/solution.py
@@ -62,7 +62,9 @@
     piece_width = stat_old.shape[0]
     row_index = lax.axis_index(GX)
     col_index = lax.axis_index(GY)
-    panel_rows = lax.all_gather(gradient, GY, axis=1, tiled=True)
+    panel_rows = jnp.concatenate(
+        lax.all_to_all(jnp.stack([gradient] * lax.axis_size(GY)), GY, 0, 0), axis=1
+    )
     outer_parts = []
     for member in range(factor):
         column_rows = spread(panel_rows, GX, col_index * factor + member)

time: 436 us -> 428 us (0.982)
  blocking collectives: 80.2 us -> 53.4 us
  waiting for transfers between devices: 323 us -> 333 us
  starting transfers between devices: 0.28 us -> 8.71 us
    all_gather x1 -> x0, blocking collectives: 26.8 us -> none  [local(): panel_rows = lax.all_gather(gradient, GY, axis=1, tiled=True)]
    all_to_all x0 -> x1, waiting for transfers between devices: none -> 8.64 us  [local(): lax.all_to_all(jnp.stack([gradient] * lax.axis_size(GY)), GY, 0, 0)]
    all_to_all x0 -> x1, starting transfers between devices: none -> 8.44 us  [local(): lax.all_to_all(jnp.stack([gradient] * lax.axis_size(GY)), GY, 0, 0)]
  transfers between devices with their start and end apart: 7 -> 8, of which waited for: 7 -> 8; matrix products, arithmetic and copies ran while one was open for 1% -> 1% of each run, Pallas kernels for 0% -> 0%
where the time goes in v1:
time: 428 us
  waiting for transfers between devices  333 us (78%)
  blocking collectives  53.4 us (12%)
  between operations  14.9 us (3%)
  matrix products  13.2 us (3%)
  starting transfers between devices  8.71 us (2%)
    all_gather x3, waiting for transfers between devices, panels(): whole_row = lax.all_gather(factor_one, GY, axis=1, tiled=True)  154 us
    psum x2, waiting for transfers between devices, spread(): array = lax.psum(array, axis)  106 us
    all_gather x2, waiting for transfers between devices, gather_axes(): filled = lax.all_gather(filled, axes[number], axis=dim, tiled=True)  62.9 us
    psum x5, blocking collectives, over_axes(): array = lax.psum(array, axis)  45.7 us
    dot_general x4, matrix products, matmul(): jnp.dot(leading, trailing, preferred_element_type=jnp.float32, precision=...  13.2 us
    all_to_all x1, waiting for transfers between devices, local(): lax.all_to_all(jnp.stack([gradient] * lax.axis_size(GY)), GY, 0, 0)  8.64 us
  transfers between devices with their start and end apart: 8, of which 8 were waited for; matrix products, arithmetic and copies ran while one was open for 1% of the time, Pallas kernels for 0%

profile of v1, /device:TPU:1, one launch (start us, length us, event | category | flops | bytes accessed | tf_op | source)
XLA Modules:
  0.0 427.7 jit_solution(2491505813099372437)
XLA Ops:
  7.2 1.4 stack.2
  8.6 8.4 %all-to-all-start = ((f32[16,128,32]{1,2,0:T(8,128)}), f32[16,128,32]{1,2,0:T(8,128)S(1)}, u32[]{:S(2)}, u32[]{:S(2)}) async-start(f32[16,128,32]{1,2,0:T(8,128)} %stack.2), calls=%async_computation | async-start | bytes 524288 | tf_op jit(solution)/shard_map/all_to_all | solution.py:66
  17.0 0.0 all-reduce.3.cloned.1.call-start
  17.1 8.6 %all-to-all-done = f32[16,128,32]{1,2,0:T(8,128)S(1)} async-done(((f32[16,128,32]{1,2,0:T(8,128)}), f32[16,128,32]{1,2,0:T(8,128)S(1)}, u32[]{:S(2)}, u32[]{:S(2)}) %all-to-all-start) | async-done | bytes 262176 | tf_op jit(solution)/shard_map/all_to_all | solution.py:66
  25.7 0.7 broadcast_select_fusion
  26.5 0.0 all-reduce.3.cloned.1.call-update
  26.5 0.0 all-reduce.5.cloned.1.call-start
  26.5 66.4 %all-reduce.3.cloned.1.call-done = f32[128,512]{0,1:T(8,128)} async-done(((f32[128,512]{0,1:T(8,128)}), f32[128,512]{0,1:T(8,128)}) %all-reduce.3.cloned.1.call-update) | async-done | bytes 262160 | tf_op jit(solution)/shard_map/psum | solution.py:27
  92.9 0.0 copy-start.2
  93.0 0.0 all-reduce.5.cloned.1.call-update
  93.0 0.0 all-gather.10.cloned.1.call-start
  93.0 0.8 copy-done.2
  93.8 0.1 copy.7
  93.9 39.7 %all-reduce.5.cloned.1.call-done = f32[128,512]{0,1:T(8,128)} async-done(((f32[128,512]{0,1:T(8,128)}), f32[128,512]{0,1:T(8,128)}) %all-reduce.5.cloned.1.call-update) | async-done | bytes 262160 | tf_op jit(solution)/shard_map/psum | solution.py:27
  133.6 2.1 multiply_reduce_fusion
  135.7 14.6 %psum.51 = f32[]{:T(128)} all-reduce(f32[]{:T(128)} %get-tuple-element.8), channel_id=1, replica_groups=mesh['gx_0'=8,'gx_1'=2,'gy_0'=4,'gy_1'=2,'gy_2'=2] {'gx_0'}, use_global_device_ids=true, to_apply=%region_3.4 | all-reduce | flops 1 | bytes 8 | tf_op jit(solution)/shard_map/psum | solution.py:33
  150.3 4.4 %psum.52 = f32[]{:T(128)} all-reduce(f32[]{:T(128)} %psum.51), channel_id=1, replica_groups=mesh['gx_0'=8,'gx_1'=2,'gy_0'=4,'gy_1'=2,'gy_2'=2] {'gx_1'}, use_global_device_ids=true, to_apply=%region_4.5 | all-reduce | flops 1 | bytes 8 | tf_op jit(solution)/shard_map/psum | solution.py:33
  154.7 9.1 %psum.53 = f32[]{:T(128)} all-reduce(f32[]{:T(128)} %psum.52), channel_id=1, replica_groups=mesh['gx_0'=8,'gx_1'=2,'gy_0'=4,'gy_1'=2,'gy_2'=2] {'gy_0'}, use_global_device_ids=true, to_apply=%region_5.6 | all-reduce | flops 1 | bytes 8 | tf_op jit(solution)/shard_map/psum | solution.py:33
  163.7 5.9 %psum.54 = f32[]{:T(128)} all-reduce(f32[]{:T(128)} %psum.53), channel_id=1, replica_groups=mesh['gx_0'=8,'gx_1'=2,'gy_0'=4,'gy_1'=2,'gy_2'=2] {'gy_1'}, use_global_device_ids=true, to_apply=%region_6.7 | all-reduce | flops 1 | bytes 8 | tf_op jit(solution)/shard_map/psum | solution.py:33
  169.6 11.8 %psum.55 = f32[]{:T(128)} all-reduce(f32[]{:T(128)} %psum.54), channel_id=1, replica_groups=mesh['gx_0'=8,'gx_1'=2,'gy_0'=4,'gy_1'=2,'gy_2'=2] {'gy_2'}, use_global_device_ids=true, to_apply=%region_7.8 | all-reduce | flops 1 | bytes 8 | tf_op jit(solution)/shard_map/psum | solution.py:33
  182.1 0.6 select_subtract_fusion
  182.7 0.0 copy-start.1
  182.7 3.9 all_gather.25
  186.6 0.0 copy-done.1
  186.6 0.0 all-gather.10.cloned.1.call-update
  186.6 0.0 all-gather.8.cloned.1.call-start
  186.7 0.5 all-gather.8.cloned.1.call-update
  187.2 0.0 all-gather.6.cloned.1.call-start
  187.3 0.5 all-gather.6.cloned.1.call-update
  187.8 0.0 all-gather.12.cloned.1.call-start
  187.9 29.4 %all-gather.10.cloned.1.call-done = f32[2048,128]{0,1:T(8,128)} async-done(((f32[256,128]{0,1:T(8,128)}), f32[2048,128]{0,1:T(8,128)}) %all-gather.10.cloned.1.call-update) | async-done | bytes 1048592 | tf_op jit(solution)/shard_map/all_gather | solution.py:15
  217.2 56.8 %all-gather.8.cloned.1.call-done = f32[128,2048]{0,1:T(8,128)} async-done(((f32[128,128]{0,1:T(8,128)}), f32[128,2048]{0,1:T(8,128)}) %all-gather.8.cloned.1.call-update) | async-done | bytes 1048592 | tf_op jit(solution)/shard_map/all_gather | solution.py:44
  274.0 3.4 fusion.3
  277.4 3.9 all_gather.27
  281.2 0.0 all-gather.12.cloned.1.call-update
  281.3 0.0 copy-start
  281.3 0.0 all-gather.14.cloned.1.call-start
  281.3 44.5 %all-gather.6.cloned.1.call-done = f32[128,2048]{0,1:T(8,128)} async-done(((f32[128,128]{0,1:T(8,128)}), f32[128,2048]{0,1:T(8,128)}) %all-gather.6.cloned.1.call-update) | async-done | bytes 1048592 | tf_op jit(solution)/shard_map/all_gather | solution.py:44
  325.9 33.6 %all-gather.12.cloned.1.call-done = f32[2048,128]{1,0:T(8,128)} async-done(((f32[256,128]{1,0:T(8,128)}), f32[2048,128]{1,0:T(8,128)}) %all-gather.12.cloned.1.call-update) | async-done | bytes 1048592 | tf_op jit(solution)/shard_map/all_gather | solution.py:15
  359.4 4.0 fusion
  363.4 0.0 all-gather.14.cloned.1.call-update
  363.5 0.7 copy.8
  364.2 53.0 %all-gather.14.cloned.1.call-done = f32[128,2048]{0,1:T(8,128)} async-done(((f32[128,128]{0,1:T(8,128)}), f32[128,2048]{0,1:T(8,128)}) %all-gather.14.cloned.1.call-update) | async-done | bytes 1048592 | tf_op jit(solution)/shard_map/all_gather | solution.py:44
  417.2 0.0 copy-done
  417.2 3.7 fusion.4
  (1 shorter events, 0.0 us)
Async XLA Ops:
  8.6 17.1 %all-to-all-start = ((f32[16,128,32]{1,2,0:T(8,128)}), f32[16,128,32]{1,2,0:T(8,128)S(1)}, u32[]{:S(2)}, u32[]{:S(2)}) async-start(f32[16,128,32]{1,2,0:T(8,128)} %stack.2), calls=%async_computation | async-start | bytes 524288 | tf_op jit(solution)/shard_map/all_to_all | solution.py:66
  17.0 75.9 %all-reduce.3.cloned.1.call-start = ((), (), s32[]{:S(2)}) async-start(), calls=%async_computation.1 | async-start | bytes 524288 | tf_op jit(solution)/shard_map/psum | solution.py:27
  26.5 107.1 %all-reduce.5.cloned.1.call-start = ((), (), s32[]{:S(2)}) async-start(), calls=%async_computation.2 | async-start | bytes 524288 | tf_op jit(solution)/shard_map/psum | solution.py:27
  92.9 0.8 copy-start.2
  93.0 124.2 %all-gather.10.cloned.1.call-start = ((), (), s32[]{:S(2)}) async-start(), calls=%async_computation.5 | async-start | bytes 1179648 | tf_op jit(solution)/shard_map/all_gather | solution.py:15
  182.7 3.9 copy-start.1
  186.6 87.3 %all-gather.8.cloned.1.call-start = ((), (), s32[]{:S(2)}) async-start(), calls=%async_computation.4 | async-start | bytes 1114112 | tf_op jit(solution)/shard_map/all_gather | solution.py:44
  187.2 138.6 %all-gather.6.cloned.1.call-start = ((), (), s32[]{:S(2)}) async-start(), calls=%async_computation.3 | async-start | bytes 1114112 | tf_op jit(solution)/shard_map/all_gather | solution.py:44
  187.8 171.6 %all-gather.12.cloned.1.call-start = ((), (), s32[]{:S(2)}) async-start(), calls=%async_computation.6 | async-start | bytes 1179648 | tf_op jit(solution)/shard_map/all_gather | solution.py:15
  281.3 135.9 %copy-start = (f32[2048,128]{0,1:T(8,128)S(1)}, f32[2048,128]{0,1:T(8,128)}, u32[]{:S(2)}) copy-start(f32[2048,128]{0,1:T(8,128)} %all-gather.10.cloned.1.call-done) | copy-start | bytes 3145732
  281.3 135.9 %all-gather.14.cloned.1.call-start = ((), (), s32[]{:S(2)}) async-start(), calls=%async_computation.7 | async-start | bytes 1114112 | tf_op jit(solution)/shard_map/all_gather | solution.py:44
Sparse Core Ops, SparseCore 0:
  26.6 66.3 all-reduce.2
  95.5 38.0 all-reduce.4
  186.8 30.4 all-gather.9
  220.4 53.5 all-gather.7
  277.2 48.6 all-gather.5
  327.5 31.8 all-gather.11
  363.6 53.5 all-gather.13
